TPU v7x, 128 devices: a whole 4x4x4 slice. The times are simulated.
128 devices in a mesh: gz: 128 (over y, z, x, core).
Axes of the slice: x: 4, y: 4, z: 4, core: 2. Of those that a mesh axis runs over, the one named last changes fastest.
Arguments:
- scores: int32 [512, 512, 512], P('gz'), may hold values from 0 to 134217727, as said below
Outputs:
- status: int32 [512, 512, 512], P('gz')
- counts: int32 [3], replicated
Inputs may be any that keep to these rules, and one draw needn't show every extreme that they name: `scores`: all values distinct: a permutation of 0 to 134217727.
All inputs are finite; a program needn't handle non-finite values.
Results may differ from a plain program's by a relative error of at most 0.000001.
Values may be sent and summed in bfloat16 or wider, within the bound.
A program may use at most 64 MiB of HBM per device.

v0:
```python
import functools

import jax
import jax.numpy as jnp
from jax import lax
from jax.experimental import pallas as pl
from jax.experimental.pallas import tpu as pltpu
from jax.sharding import PartitionSpec as P

DEPTH = 4
ROWS = 512
COLS = 512
LANES = 128
TILES = COLS // LANES
CHUNK = 32
CHUNKS = ROWS // CHUNK
STEP = 16
PAD = 8
GROUPS = (8, 4, 4)
ROOT = float(1 << 40)
MANTISSA = 23
MESH = pl.DeviceIdType.MESH


def cols(j):
    return slice(j * LANES, (j + 1) * LANES)


def shifted(tiles, by):
    shape = tiles[0].shape
    lane = lax.broadcasted_iota(jnp.int32, shape, 1)
    zero = jnp.zeros(shape, tiles[0].dtype)
    moved = [pltpu.roll(t, by % LANES, 1) for t in tiles]
    if by > 0:
        return [jnp.where(lane < by, moved[j - 1] if j else zero, moved[j]) for j in range(TILES)]
    return [
        jnp.where(lane >= LANES + by, moved[j + 1] if j < TILES - 1 else zero, moved[j])
        for j in range(TILES)
    ]


def lane_window(tiles, join):
    sides = [shifted(tiles, by) for by in (1, -1, 2, -2)]
    return [
        join(join(join(a, b), join(c, d)), t) for a, b, c, d, t in zip(*sides, tiles)
    ]


def depth_max5(p):
    m34 = jnp.maximum(p[3], p[4])
    a = jnp.maximum(p[2], m34)
    a5 = jnp.maximum(a, p[5])
    return [
        jnp.maximum(jnp.maximum(p[0], p[1]), a),
        jnp.maximum(p[1], a5),
        jnp.maximum(a5, p[6]),
        jnp.maximum(jnp.maximum(m34, p[5]), jnp.maximum(p[6], p[7])),
    ]


def row_window(ref, at, row, join):
    parts = [ref[(*at, pl.ds(row + PAD + d, STEP), slice(None))] for d in (-2, -1, 0, 1, 2)]
    return join(join(join(parts[0], parts[1]), join(parts[3], parts[4])), parts[2])


def embed(s):
    low = (s & ((1 << MANTISSA) - 1)) | (1 << MANTISSA)
    high = jnp.left_shift(jnp.ones_like(s), jnp.right_shift(s, MANTISSA))
    return low.astype(jnp.float32) * high.astype(jnp.float32)


def kernel(
    n, x_ref, out_ref, count_ref,
    x_buf, f_ref, l1_ref, l2_ref, gone_ref, t_ref, g_ref, st_ref,
    send_lo1, send_hi1, recv_lo1, recv_hi1, send_lo2, send_hi2, recv_lo2, recv_hi2,
    tally, part, parts,
    load_sem, store_sem, send_sems, recv_sems, part_send, part_recv,
):
    me = lax.axis_index("gz")
    right, left = lax.rem(me + 1, n), lax.rem(me + n - 1, n)
    keep_lo = jnp.where(me > 0, 1.0, 0.0).astype(jnp.float32)
    keep_hi = jnp.where(me < n - 1, 1.0, 0.0).astype(jnp.float32)

    partners = []
    stride = 1
    for size in GROUPS:
        place = lax.rem(lax.div(me, stride), size)
        partners.append(
            [me + (lax.rem(place + o, size) - place) * stride for o in range(1, size)]
        )
        stride *= size

    def rows_of(c):
        return pl.ds(pl.multiple_of(c * CHUNK, CHUNK), CHUNK)

    def load(c):
        return pltpu.make_async_copy(
            x_ref.at[:, rows_of(c), :], x_buf.at[:, rows_of(c), :], load_sem.at[c]
        )

    def store(c):
        return pltpu.make_async_copy(
            st_ref.at[:, rows_of(c), :], out_ref.at[:, rows_of(c), :], store_sem.at[c]
        )

    def remote(src, dst, stage, side, c, device):
        return pltpu.make_async_remote_copy(
            src_ref=src, dst_ref=dst,
            send_sem=send_sems.at[stage, side, c], recv_sem=recv_sems.at[stage, side, c],
            device_id=(device,), device_id_type=MESH,
        )

    def planes(c):
        r = rows_of(c)
        return (
            remote(f_ref.at[pl.ds(2, 2), r, :], f_ref.at[pl.ds(6, 2), r, :], 0, 1, c, left),
            remote(f_ref.at[pl.ds(4, 2), r, :], f_ref.at[pl.ds(0, 2), r, :], 0, 0, c, right),
        )

    def roots1(c):
        r = rows_of(c)
        return (
            remote(send_lo1.at[r, :], recv_hi1.at[r, :], 1, 1, c, left),
            remote(send_hi1.at[r, :], recv_lo1.at[r, :], 1, 0, c, right),
        )

    def roots2(c):
        r = rows_of(c)
        return (
            remote(send_lo2.at[r, :], recv_hi2.at[r, :], 2, 1, c, left),
            remote(send_hi2.at[r, :], recv_lo2.at[r, :], 2, 0, c, right),
        )

    def start(pair):
        for copy in pair:
            copy.start()

    def wait_recv(pair):
        for copy in pair:
            copy.wait_recv()

    def wait_send(pair):
        for copy in pair:
            copy.wait_send()

    def loop(first, last, body):
        def step(i, carry):
            body(i)
            return carry
        lax.fori_loop(first, last, step, 0)

    def over_rows(c, body):
        loop(0, CHUNK // STEP, lambda i: body(pl.multiple_of(c * CHUNK + i * STEP, STEP)))

    loop(0, CHUNKS, lambda c: load(c).start())
    barrier = pltpu.get_barrier_semaphore()
    greeted = [left, right, *(p for group in partners for p in group)]
    for other in greeted:
        pl.semaphore_signal(barrier, inc=1, device_id=(other,), device_id_type=MESH)
    for j in range(TILES):
        for edge in (slice(0, PAD), slice(PAD + ROWS, 2 * PAD + ROWS)):
            for k in range(DEPTH):
                t_ref[k, j, edge, :] = jnp.zeros((PAD, LANES), jnp.float32)
            g_ref[j, edge, :] = jnp.zeros((PAD, LANES), jnp.int32)
    for k in range(3):
        tally[k] = jnp.zeros((8, LANES), jnp.int32)

    def prepare(c):
        load(c).wait()

        def body(row):
            for k in range(DEPTH):
                for j in range(TILES):
                    at = (pl.ds(row, STEP), cols(j))
                    f_ref[(2 + k,) + at] = embed(x_buf[(k,) + at])
        over_rows(c, body)

    def send_planes(c):
        prepare(c)
        start(planes(c))

    prepare(0)
    pl.semaphore_wait(barrier, len(greeted))
    start(planes(0))
    loop(1, CHUNKS, send_planes)

    def rounds(first, second, arrive, leave):
        arrive(0)
        over_rows(0, first)

        def step(c):
            arrive(c)

            def body(row):
                second(pl.multiple_of(row - CHUNK, STEP))
                first(row)
            over_rows(c, body)
            leave(c - 1)
        loop(1, CHUNKS, step)
        over_rows(CHUNKS - 1, second)
        leave(CHUNKS - 1)

    def add_count(k, flags):
        while len(flags) > 1:
            flags = [a + b for a, b in zip(flags[::2], flags[1::2])]
        tally[k] += flags[0][:8] + flags[0][8:]

    def laterals(outs):
        for k in range(DEPTH):
            yield k, lane_window([o[k] for o in outs], jnp.maximum)

    def put(row, outs):
        for k, tiles in laterals(outs):
            for j, t in enumerate(tiles):
                t_ref[k, j, pl.ds(row + PAD, STEP), :] = t

    def first1(row):
        outs = []
        for j in range(TILES):
            at = (pl.ds(row, STEP), cols(j))
            p = [f_ref[(k,) + at] for k in range(8)]
            for k, keep in ((0, keep_lo), (1, keep_lo), (6, keep_hi), (7, keep_hi)):
                p[k] = p[k] * keep
                f_ref[(k,) + at] = p[k]
            outs.append(depth_max5(p))
        put(row, outs)

    def second1(row):
        flags = []
        for j in range(TILES):
            at = (pl.ds(row, STEP), cols(j))
            roots = []
            for k in range(DEPTH):
                s = f_ref[(2 + k,) + at]
                root = row_window(t_ref, (k, j), row, jnp.maximum) == s
                l1_ref[(k,) + at] = jnp.where(root, ROOT, s)
                flags.append(jnp.where(root, 0, 1))
                roots.append(root)
            lo = jnp.zeros((STEP, LANES), jnp.float32)
            hi = lo
            for k in range(DEPTH):
                hi = jnp.where(roots[k], float(DEPTH - k), hi)
                lo = jnp.where(roots[DEPTH - 1 - k], float(DEPTH - k), lo)
            send_lo1[at] = lo.astype(jnp.bfloat16)
            send_hi1[at] = hi.astype(jnp.bfloat16)
        add_count(0, flags)

    rounds(first1, second1, lambda c: wait_recv(planes(c)), lambda c: start(roots1(c)))

    def first2(row):
        outs, marks = [], []
        for j in range(TILES):
            at = (pl.ds(row, STEP), cols(j))
            d_lo = recv_lo1[at].astype(jnp.float32) * keep_lo
            d_hi = recv_hi1[at].astype(jnp.float32) * keep_hi
            mine = [l1_ref[(k,) + at] for k in range(DEPTH)]
            outs.append(depth_max5([
                jnp.where(d_lo == 2.0, ROOT, f_ref[(0,) + at]),
                jnp.where(d_lo == 1.0, ROOT, f_ref[(1,) + at]),
                *mine,
                jnp.where(d_hi == 1.0, ROOT, f_ref[(6,) + at]),
                jnp.where(d_hi == 2.0, ROOT, f_ref[(7,) + at]),
            ]))
            mark = jnp.where(d_lo > 3.5, 1, jnp.where(d_lo > 0.5, 3, 0))
            mark |= jnp.where(d_hi > 3.5, 8, jnp.where(d_hi > 0.5, 12, 0))
            for value, bits in zip(mine, (3, 2, 4, 12)):
                mark |= jnp.where(value == ROOT, bits, 0)
            marks.append(mark)
        put(row, outs)
        for j, t in enumerate(lane_window(marks, jnp.bitwise_or)):
            g_ref[j, pl.ds(row + PAD, STEP), :] = t

    def second2(row):
        flags = []
        for j in range(TILES):
            at = (pl.ds(row, STEP), cols(j))
            roots = []
            for k in range(DEPTH):
                l = l1_ref[(k,) + at]
                top = row_window(t_ref, (k, j), row, jnp.maximum)
                root, near = top == l, top >= ROOT
                value = jnp.where(root, ROOT, jnp.where(near, 0.0, l))
                l2_ref[(k,) + at] = value
                flags.append(jnp.where(root | near, 0, 1))
                roots.append(root)
            gone_ref[at] = row_window(g_ref, (j,), row, jnp.bitwise_or)
            lo = jnp.where(roots[0], 1.0, jnp.where(roots[1], 2.0, 0.0))
            hi = jnp.where(roots[3], 1.0, jnp.where(roots[2], 2.0, 0.0))
            send_lo2[at] = lo.astype(jnp.bfloat16)
            send_hi2[at] = hi.astype(jnp.bfloat16)
        add_count(1, flags)

    rounds(first2, second2, lambda c: wait_recv(roots1(c)), lambda c: start(roots2(c)))

    def first3(row):
        outs = []
        for j in range(TILES):
            at = (pl.ds(row, STEP), cols(j))
            d_lo = recv_lo2[at].astype(jnp.float32) * keep_lo
            d_hi = recv_hi2[at].astype(jnp.float32) * keep_hi
            gone = gone_ref[at]

            def halo(k, bit, is_root):
                left_over = jnp.where((gone & bit) == 0, f_ref[(k,) + at], 0.0)
                return jnp.where(is_root, ROOT, left_over)

            outs.append(depth_max5([
                halo(0, 1, d_lo == 2.0), halo(1, 2, d_lo == 1.0),
                *(l2_ref[(k,) + at] for k in range(DEPTH)),
                halo(6, 4, d_hi == 1.0), halo(7, 8, d_hi == 2.0),
            ]))
        put(row, outs)

    def second3(row):
        flags = []
        for j in range(TILES):
            at = (pl.ds(row, STEP), cols(j))
            for k in range(DEPTH):
                top = row_window(t_ref, (k, j), row, jnp.maximum)
                root, near = top == l2_ref[(k,) + at], top >= ROOT
                state = jnp.where(root, 1.0, jnp.where(near, 2.0, 0.0))
                st_ref[(k,) + at] = state.astype(jnp.bfloat16)
                flags.append(jnp.where(root | near, 0, 1))
        add_count(2, flags)

    rounds(first3, second3, lambda c: wait_recv(roots2(c)), lambda c: store(c).start())

    for k in range(3):
        part[0, k:k + 1, :] = jnp.sum(tally[k], axis=0, keepdims=True)
    part[0, 3:8, :] = jnp.zeros((5, LANES), jnp.int32)
    slot = 0
    for stage, group in enumerate(partners):
        copies = [
            pltpu.make_async_remote_copy(
                src_ref=part.at[stage], dst_ref=parts.at[slot + o],
                send_sem=part_send.at[slot + o], recv_sem=part_recv.at[slot + o],
                device_id=(other,), device_id_type=MESH,
            )
            for o, other in enumerate(group)
        ]
        start(copies)
        total = part[stage]
        for o, copy in enumerate(copies):
            copy.wait_recv()
            total = total + parts[slot + o]
        part[stage + 1] = total
        wait_send(copies)
        slot += len(group)
    for k in range(3):
        count_ref[k] = jnp.sum(part[len(GROUPS), k:k + 1, :])

    def drain(c):
        wait_send(planes(c))
        wait_send(roots1(c))
        wait_send(roots2(c))
        store(c).wait()

    loop(0, CHUNKS, drain)


def shards(n, scores):
    slab = (DEPTH, ROWS, COLS)
    column = pltpu.VMEM((ROWS, COLS), jnp.bfloat16)
    slots = sum(GROUPS) - len(GROUPS)
    status, counts = pl.pallas_call(
        functools.partial(kernel, n),
        out_shape=(
            jax.ShapeDtypeStruct(slab, jnp.bfloat16),
            jax.ShapeDtypeStruct((3,), jnp.int32),
        ),
        in_specs=[pl.BlockSpec(memory_space=pl.ANY)],
        out_specs=(
            pl.BlockSpec(memory_space=pl.ANY),
            pl.BlockSpec(memory_space=pltpu.SMEM),
        ),
        scratch_shapes=[
            pltpu.VMEM(slab, jnp.int32),
            pltpu.VMEM((2 * DEPTH, ROWS, COLS), jnp.float32),
            pltpu.VMEM(slab, jnp.float32),
            pltpu.VMEM(slab, jnp.float32),
            pltpu.VMEM((ROWS, COLS), jnp.int32),
            pltpu.VMEM((DEPTH, TILES, ROWS + 2 * PAD, LANES), jnp.float32),
            pltpu.VMEM((TILES, ROWS + 2 * PAD, LANES), jnp.int32),
            pltpu.VMEM(slab, jnp.bfloat16),
            *[column] * 8,
            pltpu.VMEM((3, 8, LANES), jnp.int32),
            pltpu.VMEM((len(GROUPS) + 1, 8, LANES), jnp.int32),
            pltpu.VMEM((slots, 8, LANES), jnp.int32),
            pltpu.SemaphoreType.DMA((CHUNKS,)),
            pltpu.SemaphoreType.DMA((CHUNKS,)),
            pltpu.SemaphoreType.DMA((3, 2, CHUNKS)),
            pltpu.SemaphoreType.DMA((3, 2, CHUNKS)),
            pltpu.SemaphoreType.DMA((slots,)),
            pltpu.SemaphoreType.DMA((slots,)),
        ],
        compiler_params=pltpu.CompilerParams(
            collective_id=0, has_side_effects=True, vmem_limit_bytes=56 << 20
        ),
    )(scores)
    return status.astype(jnp.int32), counts


def solution(mesh):
    n = mesh.shape["gz"]
    return jax.shard_map(
        functools.partial(shards, n),
        mesh=mesh,
        in_specs=(P("gz", None, None),),
        out_specs=(P("gz", None, None), P()),
        check_vma=False,
    )
```

profile of v0, /device:TPU:1, one launch (start us, length us, event | category | flops | bytes accessed | tf_op | source)
XLA Modules:
  0.0 73.1 jit_solution(6351456766169942778)
XLA Ops:
  0.6 67.7 %shard_map.30 = (bf16[4,512,512]{2,1,0:T(8,128)(2,1)}, s32[3]{0:T(128)}) custom-call(s32[4,512,512]{2,1,0:T(8,128)} %x_ref.1), custom_call_target="tpu_custom_call" | custom-call | tf_op jit(solution)/shard_map/pallas_call | solution.py:365
  68.3 0.0 copy-start
  68.3 4.3 %convert_element_type.3 = s32[4,512,512]{2,1,0:T(8,128)} convert(bf16[4,512,512]{2,1,0:T(8,128)(2,1)} %get-tuple-element.4) | non-fusion elementwise | flops 1048576 | bytes 6291456 | tf_op jit(solution)/shard_map/convert_element_type | solution.py:400
  72.6 0.0 copy-done
  72.6 0.5 copy.4
Async XLA Ops:
  68.3 4.3 %copy-start = (s32[3]{0:T(128)S(1)}, s32[3]{0:T(128)}, u32[]{:S(2)}) copy-start(s32[3]{0:T(128)} %get-tuple-element.9) | copy-start | bytes 40
where the time goes:
time: 73.6 us; the launch traced here: 73.1 us
  Pallas kernels  67.7 us (92%)
  other arithmetic  4.26 us (6%)
    pallas_call x1, Pallas kernels, shards(): pl.pallas_call(functools.partial(kernel, n), out_shape=(jax.ShapeDtypeStr...  67.7 us
    convert_element_type x1, other arithmetic, shards(): return (status.astype(jnp.int32), counts)  4.26 us

commit v1 on v0

--- a/solution.py
+++ b/solution.py
@@ -11,7 +11,8 @@
 ROWS = 512
 COLS = 512
 LANES = 128
-TILES = COLS // LANES
+TILES = 4
+BLOCK = LANES // TILES
 CHUNK = 32
 CHUNKS = ROWS // CHUNK
 STEP = 16
@@ -26,24 +27,63 @@
     return slice(j * LANES, (j + 1) * LANES)
 
 
-def shifted(tiles, by):
-    shape = tiles[0].shape
-    lane = lax.broadcasted_iota(jnp.int32, shape, 1)
-    zero = jnp.zeros(shape, tiles[0].dtype)
-    moved = [pltpu.roll(t, by % LANES, 1) for t in tiles]
-    if by > 0:
-        return [jnp.where(lane < by, moved[j - 1] if j else zero, moved[j]) for j in range(TILES)]
+def gather(x, index):
+    halves = [
+        jnp.take_along_axis(x[r:r + 8], index, axis=1, mode="promise_in_bounds")
+        for r in range(0, x.shape[0], 8)
+    ]
+    return jnp.concatenate(halves, axis=0)
+
+
+def lane_of(height):
+    return lax.broadcasted_iota(jnp.int32, (height, LANES), 1)
+
+
+def by_block(tiles, source):
+    block = lane_of(tiles[0].shape[0]) // BLOCK
+    out = []
+    for a in range(TILES):
+        t = tiles[source(TILES - 1, a)]
+        for p in range(TILES - 1):
+            t = jnp.where(block == p, tiles[source(p, a)], t)
+        out.append(t)
+    return out
+
+
+def interleave(tiles):
+    lane = lane_of(8)
+    sorted_ = [
+        gather(t, (lane % BLOCK) * TILES + (lane // BLOCK + TILES - s) % TILES)
+        for s, t in enumerate(tiles)
+    ]
+    mixed = by_block(sorted_, lambda p, j: (p - j) % TILES)
+    return [pltpu.roll(t, LANES - BLOCK * j, 1) if j else t for j, t in enumerate(mixed)]
+
+
+def natural(tiles):
+    lane = lane_of(8)
+    turned = [pltpu.roll(t, BLOCK * j, 1) if j else t for j, t in enumerate(tiles)]
+    mixed = by_block(turned, lambda p, s: (p - s) % TILES)
     return [
-        jnp.where(lane >= LANES + by, moved[j + 1] if j < TILES - 1 else zero, moved[j])
-        for j in range(TILES)
+        gather(t, BLOCK * ((lane % TILES + s) % TILES) + lane // TILES)
+        for s, t in enumerate(mixed)
     ]
 
 
-def lane_window(tiles, join):
-    sides = [shifted(tiles, by) for by in (1, -1, 2, -2)]
-    return [
-        join(join(join(a, b), join(c, d)), t) for a, b, c, d, t in zip(*sides, tiles)
-    ]
+def column_sides(t):
+    lane = lane_of(t[0].shape[0])
+    zero = jnp.zeros(t[0].shape, t[0].dtype)
+    before = [jnp.where(lane == 0, zero, pltpu.roll(t[j], 1, 1)) for j in (2, 3)]
+    after = [jnp.where(lane == LANES - 1, zero, pltpu.roll(t[j], LANES - 1, 1)) for j in (0, 1)]
+    return (*before, *after)
+
+
+def column_window(t, sides, join):
+    r2, r3, l0, l1 = sides
+    m12 = join(t[1], t[2])
+    m012, m123 = join(t[0], m12), join(m12, t[3])
+    whole = join(m012, t[3])
+    return [join(m012, join(r2, r3)), join(whole, r3), join(whole, l0), join(m123, join(l0, l1))]
 
 
 def depth_max5(p):
@@ -100,7 +140,7 @@
 
     def store(c):
         return pltpu.make_async_copy(
-            st_ref.at[:, rows_of(c), :], out_ref.at[:, rows_of(c), :], store_sem.at[c]
+            st_ref.at[rows_of(c), :], out_ref.at[rows_of(c), :], store_sem.at[c]
         )
 
     def remote(src, dst, stage, side, c, device):
@@ -170,9 +210,9 @@
 
         def body(row):
             for k in range(DEPTH):
-                for j in range(TILES):
-                    at = (pl.ds(row, STEP), cols(j))
-                    f_ref[(2 + k,) + at] = embed(x_buf[(k,) + at])
+                tiles = [x_buf[k, pl.ds(row, STEP), cols(j)] for j in range(TILES)]
+                for j, t in enumerate(interleave(tiles)):
+                    f_ref[2 + k, pl.ds(row, STEP), cols(j)] = embed(t)
         over_rows(c, body)
 
     def send_planes(c):
@@ -186,14 +226,15 @@
 
     def rounds(first, second, arrive, leave):
         arrive(0)
-        over_rows(0, first)
+        over_rows(0, lambda row: first(row)())
 
         def step(c):
             arrive(c)
 
             def body(row):
+                finish = first(row)
                 second(pl.multiple_of(row - CHUNK, STEP))
-                first(row)
+                finish()
             over_rows(c, body)
             leave(c - 1)
         loop(1, CHUNKS, step)
@@ -205,25 +246,31 @@
             flags = [a + b for a, b in zip(flags[::2], flags[1::2])]
         tally[k] += flags[0][:8] + flags[0][8:]
 
-    def laterals(outs):
+    def sides_of(outs):
+        return [column_sides([o[k] for o in outs]) for k in range(DEPTH)]
+
+    def put(row, outs, sides):
         for k in range(DEPTH):
-            yield k, lane_window([o[k] for o in outs], jnp.maximum)
-
-    def put(row, outs):
-        for k, tiles in laterals(outs):
+            tiles = column_window([o[k] for o in outs], sides[k], jnp.maximum)
             for j, t in enumerate(tiles):
                 t_ref[k, j, pl.ds(row + PAD, STEP), :] = t
 
     def first1(row):
-        outs = []
+        outs, halos = [], []
         for j in range(TILES):
             at = (pl.ds(row, STEP), cols(j))
             p = [f_ref[(k,) + at] for k in range(8)]
             for k, keep in ((0, keep_lo), (1, keep_lo), (6, keep_hi), (7, keep_hi)):
                 p[k] = p[k] * keep
-                f_ref[(k,) + at] = p[k]
+                halos.append(((k,) + at, p[k]))
             outs.append(depth_max5(p))
-        put(row, outs)
+        sides = sides_of(outs)
+
+        def finish():
+            for at, value in halos:
+                f_ref[at] = value
+            put(row, outs, sides)
+        return finish
 
     def second1(row):
         flags = []
@@ -266,9 +313,13 @@
             for value, bits in zip(mine, (3, 2, 4, 12)):
                 mark |= jnp.where(value == ROOT, bits, 0)
             marks.append(mark)
-        put(row, outs)
-        for j, t in enumerate(lane_window(marks, jnp.bitwise_or)):
-            g_ref[j, pl.ds(row + PAD, STEP), :] = t
+        sides, mark_sides = sides_of(outs), column_sides(marks)
+
+        def finish():
+            put(row, outs, sides)
+            for j, t in enumerate(column_window(marks, mark_sides, jnp.bitwise_or)):
+                g_ref[j, pl.ds(row + PAD, STEP), :] = t
+        return finish
 
     def second2(row):
         flags = []
@@ -309,18 +360,23 @@
                 *(l2_ref[(k,) + at] for k in range(DEPTH)),
                 halo(6, 4, d_hi == 1.0), halo(7, 8, d_hi == 2.0),
             ]))
-        put(row, outs)
+        sides = sides_of(outs)
+        return lambda: put(row, outs, sides)
 
     def second3(row):
-        flags = []
-        for j in range(TILES):
-            at = (pl.ds(row, STEP), cols(j))
+        flags, words = [], []
+        for j in range(TILES):
+            at = (pl.ds(row, STEP), cols(j))
+            word = None
             for k in range(DEPTH):
                 top = row_window(t_ref, (k, j), row, jnp.maximum)
                 root, near = top == l2_ref[(k,) + at], top >= ROOT
-                state = jnp.where(root, 1.0, jnp.where(near, 2.0, 0.0))
-                st_ref[(k,) + at] = state.astype(jnp.bfloat16)
+                state = jnp.where(root, 1 << 2 * k, jnp.where(near, 2 << 2 * k, 0))
+                word = state if word is None else word | state
                 flags.append(jnp.where(root | near, 0, 1))
+            words.append(word)
+        for j, t in enumerate(natural(words)):
+            st_ref[pl.ds(row, STEP), cols(j)] = t
         add_count(2, flags)
 
     rounds(first3, second3, lambda c: wait_recv(roots2(c)), lambda c: store(c).start())
@@ -362,10 +418,10 @@
     slab = (DEPTH, ROWS, COLS)
     column = pltpu.VMEM((ROWS, COLS), jnp.bfloat16)
     slots = sum(GROUPS) - len(GROUPS)
-    status, counts = pl.pallas_call(
+    words, counts = pl.pallas_call(
         functools.partial(kernel, n),
         out_shape=(
-            jax.ShapeDtypeStruct(slab, jnp.bfloat16),
+            jax.ShapeDtypeStruct((ROWS, COLS), jnp.int32),
             jax.ShapeDtypeStruct((3,), jnp.int32),
         ),
         in_specs=[pl.BlockSpec(memory_space=pl.ANY)],
@@ -381,7 +437,7 @@
             pltpu.VMEM((ROWS, COLS), jnp.int32),
             pltpu.VMEM((DEPTH, TILES, ROWS + 2 * PAD, LANES), jnp.float32),
             pltpu.VMEM((TILES, ROWS + 2 * PAD, LANES), jnp.int32),
-            pltpu.VMEM(slab, jnp.bfloat16),
+            pltpu.VMEM((ROWS, COLS), jnp.int32),
             *[column] * 8,
             pltpu.VMEM((3, 8, LANES), jnp.int32),
             pltpu.VMEM((len(GROUPS) + 1, 8, LANES), jnp.int32),
@@ -397,7 +453,8 @@
             collective_id=0, has_side_effects=True, vmem_limit_bytes=56 << 20
         ),
     )(scores)
-    return status.astype(jnp.int32), counts
+    plane = lax.broadcasted_iota(jnp.int32, slab, 0)
+    return jnp.right_shift(jnp.right_shift(words[None], plane), plane) & 3, counts
 
 
 def solution(mesh):

time: 73.6 us -> 67.9 us (0.923)
  Pallas kernels: 67.7 us -> 62.4 us
    pallas_call x1, Pallas kernels: 67.7 us -> 62.4 us  [shards(): pl.pallas_call(functools.partial(kernel, n), out_shape=(jax.ShapeDtypeStr...]
    convert_element_type x1 -> x0, other arithmetic: 4.26 us -> none  [shards(): return (status.astype(jnp.int32), counts)]
    and x0 -> x1, other arithmetic: none -> 3.84 us  [shards(): jnp.right_shift(jnp.right_shift(words[None], plane), plane) & 3]
where the time goes in v1:
time: 67.9 us; the launch traced here: 67.4 us
  Pallas kernels  62.4 us (92%)
  other arithmetic  3.84 us (6%)
    pallas_call x1, Pallas kernels, shards(): pl.pallas_call(functools.partial(kernel, n), out_shape=(jax.ShapeDtypeStr...  62.4 us
    and x1, other arithmetic, shards(): jnp.right_shift(jnp.right_shift(words[None], plane), plane) & 3  3.84 us

profile of v1, /device:TPU:1, one launch (start us, length us, event | category | flops | bytes accessed | tf_op | source)
XLA Modules:
  0.0 67.4 jit_solution(16600195631927836156)
XLA Ops:
  0.6 62.4 %shard_map.30 = (s32[512,512]{1,0:T(8,128)}, s32[3]{0:T(128)}) custom-call(s32[4,512,512]{2,1,0:T(8,128)} %x_ref.1), custom_call_target="tpu_custom_call" | custom-call | tf_op jit(solution)/shard_map/pallas_call | solution.py:421
  63.0 0.0 copy-start
  63.0 3.8 %shift-right-arithmetic_and_fusion = s32[4,512,512]{2,1,0:T(8,128)} fusion(s32[512,512]{1,0:T(8,128)} %get-tuple-element.4), kind=kLoop, calls=%fused_computation | loop fusion | flops 3145728 | bytes 5242880 | tf_op jit(solution)/shard_map/and | solution.py:457
  66.9 0.0 copy-done
  66.9 0.5 copy.4
Async XLA Ops:
  63.0 3.9 %copy-start = (s32[3]{0:T(128)S(1)}, s32[3]{0:T(128)}, u32[]{:S(2)}) copy-start(s32[3]{0:T(128)} %get-tuple-element.9) | copy-start | bytes 40

commit v2 on v1

--- a/solution.py
+++ b/solution.py
@@ -16,10 +16,15 @@
 CHUNK = 32
 CHUNKS = ROWS // CHUNK
 STEP = 16
+OUT_ROWS = 256
 PAD = 8
-GROUPS = (8, 4, 4)
+GROUPS = (8, 16)
 ROOT = float(1 << 40)
 MANTISSA = 23
+BITS = 27
+SPARE = 32 - BITS
+CARRIERS = 6
+SENT = 2 * TILES - 1
 MESH = pl.DeviceIdType.MESH
 
 
@@ -105,15 +110,30 @@
 
 def embed(s):
     low = (s & ((1 << MANTISSA) - 1)) | (1 << MANTISSA)
-    high = jnp.left_shift(jnp.ones_like(s), jnp.right_shift(s, MANTISSA))
-    return low.astype(jnp.float32) * high.astype(jnp.float32)
+    exponent = jnp.right_shift(s, MANTISSA) & ((1 << (BITS - MANTISSA)) - 1)
+    return low.astype(jnp.float32) * jnp.left_shift(jnp.ones_like(s), exponent).astype(jnp.float32)
+
+
+def pack(tiles):
+    *words, spare = tiles
+    for i in range(CARRIERS):
+        words[i] = words[i] | jnp.left_shift(jnp.right_shift(spare, SPARE * i), BITS)
+    return words
+
+
+def unpack(words):
+    spare = None
+    for i in range(CARRIERS):
+        bits = jnp.left_shift(lax.shift_right_logical(words[i], BITS), SPARE * i)
+        spare = bits if spare is None else spare | bits
+    return [*words, spare]
 
 
 def kernel(
     n, x_ref, out_ref, count_ref,
     x_buf, f_ref, l1_ref, l2_ref, gone_ref, t_ref, g_ref, st_ref,
     send_lo1, send_hi1, recv_lo1, recv_hi1, send_lo2, send_hi2, recv_lo2, recv_hi2,
-    tally, part, parts,
+    pack_lo, pack_hi, packed_lo, packed_hi, tally, part, parts,
     load_sem, store_sem, send_sems, recv_sems, part_send, part_recv,
 ):
     me = lax.axis_index("gz")
@@ -153,8 +173,8 @@
     def planes(c):
         r = rows_of(c)
         return (
-            remote(f_ref.at[pl.ds(2, 2), r, :], f_ref.at[pl.ds(6, 2), r, :], 0, 1, c, left),
-            remote(f_ref.at[pl.ds(4, 2), r, :], f_ref.at[pl.ds(0, 2), r, :], 0, 0, c, right),
+            remote(pack_lo.at[r, :], packed_hi.at[r, :], 0, 1, c, left),
+            remote(pack_hi.at[r, :], packed_lo.at[r, :], 0, 0, c, right),
         )
 
     def roots1(c):
@@ -209,10 +229,15 @@
         load(c).wait()
 
         def body(row):
+            own = []
             for k in range(DEPTH):
                 tiles = [x_buf[k, pl.ds(row, STEP), cols(j)] for j in range(TILES)]
-                for j, t in enumerate(interleave(tiles)):
-                    f_ref[2 + k, pl.ds(row, STEP), cols(j)] = embed(t)
+                own += interleave(tiles)
+            for ref, tiles in ((pack_lo, own[:2 * TILES]), (pack_hi, own[2 * TILES:])):
+                for i, word in enumerate(pack(tiles)):
+                    ref[pl.ds(row, STEP), cols(i)] = word
+            for i, t in enumerate(own):
+                f_ref[2 + i // TILES, pl.ds(row, STEP), cols(i % TILES)] = embed(t)
         over_rows(c, body)
 
     def send_planes(c):
@@ -257,12 +282,18 @@
 
     def first1(row):
         outs, halos = [], []
+        rows = pl.ds(row, STEP)
+        low, high = (
+            [embed(t) * keep for t in unpack([ref[rows, cols(i)] for i in range(SENT)])]
+            for ref, keep in ((packed_lo, keep_lo), (packed_hi, keep_hi))
+        )
         for j in range(TILES):
-            at = (pl.ds(row, STEP), cols(j))
-            p = [f_ref[(k,) + at] for k in range(8)]
-            for k, keep in ((0, keep_lo), (1, keep_lo), (6, keep_hi), (7, keep_hi)):
-                p[k] = p[k] * keep
-                halos.append(((k,) + at, p[k]))
+            at = (rows, cols(j))
+            p = [
+                low[j], low[TILES + j], *(f_ref[(k,) + at] for k in range(2, 6)),
+                high[j], high[TILES + j],
+            ]
+            halos += [((k,) + at, p[k]) for k in (0, 1, 6, 7)]
             outs.append(depth_max5(p))
         sides = sides_of(outs)
 
@@ -412,6 +443,14 @@
         store(c).wait()
 
     loop(0, CHUNKS, drain)
+
+
+def expand(word_ref, count_ref, out_ref, count_out_ref):
+    words = word_ref[...]
+    for k in range(DEPTH):
+        out_ref[k] = jnp.right_shift(words, 2 * k) & 3
+    for k in range(3):
+        count_out_ref[k] = count_ref[k]
 
 
 def shards(n, scores):
@@ -439,6 +478,7 @@
             pltpu.VMEM((TILES, ROWS + 2 * PAD, LANES), jnp.int32),
             pltpu.VMEM((ROWS, COLS), jnp.int32),
             *[column] * 8,
+            *[pltpu.VMEM((ROWS, SENT * LANES), jnp.int32)] * 4,
             pltpu.VMEM((3, 8, LANES), jnp.int32),
             pltpu.VMEM((len(GROUPS) + 1, 8, LANES), jnp.int32),
             pltpu.VMEM((slots, 8, LANES), jnp.int32),
@@ -453,8 +493,22 @@
             collective_id=0, has_side_effects=True, vmem_limit_bytes=56 << 20
         ),
     )(scores)
-    plane = lax.broadcasted_iota(jnp.int32, slab, 0)
-    return jnp.right_shift(jnp.right_shift(words[None], plane), plane) & 3, counts
+    return pl.pallas_call(
+        expand,
+        out_shape=(
+            jax.ShapeDtypeStruct(slab, jnp.int32),
+            jax.ShapeDtypeStruct((3,), jnp.int32),
+        ),
+        grid=(ROWS // OUT_ROWS,),
+        in_specs=[
+            pl.BlockSpec((OUT_ROWS, COLS), lambda i: (i, 0)),
+            pl.BlockSpec(memory_space=pltpu.SMEM),
+        ],
+        out_specs=(
+            pl.BlockSpec((DEPTH, OUT_ROWS, COLS), lambda i: (0, i, 0)),
+            pl.BlockSpec(memory_space=pltpu.SMEM),
+        ),
+    )(words, counts)
 
 
 def solution(mesh):

time: 67.9 us -> 62.3 us (0.918)
  other arithmetic: 3.84 us -> 0 us
  Pallas kernels: 62.4 us -> 61.5 us
    pallas_call x1, Pallas kernels: 62.4 us -> 58.3 us  [shards(): pl.pallas_call(functools.partial(kernel, n), out_shape=(jax.ShapeDtypeStr...]
    and x1 -> x0, other arithmetic: 3.84 us -> none  [shards(): jnp.right_shift(jnp.right_shift(words[None], plane), plane) & 3]
    pallas_call x0 -> x1, Pallas kernels: none -> 3.27 us  [shards(): pl.pallas_call(expand, out_shape=(jax.ShapeDtypeStruct(slab, jnp.int32),...]
where the time goes in v2:
time: 62.3 us; the launch traced here: 62.2 us
  Pallas kernels  61.5 us (99%)
  between operations  0.64 us (1%)
    pallas_call x1, Pallas kernels, shards(): pl.pallas_call(functools.partial(kernel, n), out_shape=(jax.ShapeDtypeStr...  58.3 us
    pallas_call x1, Pallas kernels, shards(): pl.pallas_call(expand, out_shape=(jax.ShapeDtypeStruct(slab, jnp.int32),...  3.27 us

profile of v2, /device:TPU:1, one launch (start us, length us, event | category | flops | bytes accessed | tf_op | source)
XLA Modules:
  0.0 62.2 jit_solution(12524390922695647692)
XLA Ops:
  0.6 58.3 %shard_map.30 = (s32[512,512]{1,0:T(8,128)}, s32[3]{0:T(128)}) custom-call(s32[4,512,512]{2,1,0:T(8,128)} %x_ref.1), custom_call_target="tpu_custom_call" | custom-call | tf_op jit(solution)/shard_map/pallas_call | solution.py:460
  58.9 3.3 %shard_map.31 = (s32[4,512,512]{2,1,0:T(8,128)}, s32[3]{0:T(128)}) custom-call(s32[512,512]{1,0:T(8,128)} %get-tuple-element.4.word_ref, s32[3]{0:T(128)} %get-tuple-element.5.count_ref), custom_call_target="tpu_custom_call" | custom-call | tf_op jit(solution)/shard_map/pallas_call | solution.py:496

commit v3 on v2

--- a/solution.py
+++ b/solution.py
@@ -138,8 +138,7 @@
 ):
     me = lax.axis_index("gz")
     right, left = lax.rem(me + 1, n), lax.rem(me + n - 1, n)
-    keep_lo = jnp.where(me > 0, 1.0, 0.0).astype(jnp.float32)
-    keep_hi = jnp.where(me < n - 1, 1.0, 0.0).astype(jnp.float32)
+    has_left, has_right = me > 0, me < n - 1
 
     partners = []
     stride = 1
@@ -191,17 +190,18 @@
             remote(send_hi2.at[r, :], recv_lo2.at[r, :], 2, 0, c, right),
         )
 
+    def sided(on_left, on_right):
+        pl.when(has_left)(on_left)
+        pl.when(has_right)(on_right)
+
     def start(pair):
-        for copy in pair:
-            copy.start()
+        sided(pair[0].start, pair[1].start)
 
     def wait_recv(pair):
-        for copy in pair:
-            copy.wait_recv()
+        sided(pair[1].wait_recv, pair[0].wait_recv)
 
     def wait_send(pair):
-        for copy in pair:
-            copy.wait_send()
+        sided(pair[0].wait_send, pair[1].wait_send)
 
     def loop(first, last, body):
         def step(i, carry):
@@ -214,9 +214,26 @@
 
     loop(0, CHUNKS, lambda c: load(c).start())
     barrier = pltpu.get_barrier_semaphore()
-    greeted = [left, right, *(p for group in partners for p in group)]
+
+    def greet(other):
+        pl.semaphore_signal(barrier, inc=1, device_id=(other,), device_id_type=MESH)
+
+    sided(lambda: greet(left), lambda: greet(right))
+    greeted = [p for group in partners for p in group]
     for other in greeted:
-        pl.semaphore_signal(barrier, inc=1, device_id=(other,), device_id_type=MESH)
+        greet(other)
+
+    def outside(*refs):
+        def fill():
+            def body(i):
+                rows = pl.ds(pl.multiple_of(i * CHUNK, CHUNK), CHUNK)
+                for ref in refs:
+                    ref[rows, :] = jnp.zeros((CHUNK, ref.shape[1]), ref.dtype)
+            loop(0, CHUNKS, body)
+        return fill
+
+    pl.when(jnp.logical_not(has_left))(outside(packed_lo, recv_lo1, recv_lo2))
+    pl.when(jnp.logical_not(has_right))(outside(packed_hi, recv_hi1, recv_hi2))
     for j in range(TILES):
         for edge in (slice(0, PAD), slice(PAD + ROWS, 2 * PAD + ROWS)):
             for k in range(DEPTH):
@@ -245,7 +262,8 @@
         start(planes(c))
 
     prepare(0)
-    pl.semaphore_wait(barrier, len(greeted))
+    neighbours = has_left.astype(jnp.int32) + has_right.astype(jnp.int32)
+    pl.semaphore_wait(barrier, neighbours + len(greeted))
     start(planes(0))
     loop(1, CHUNKS, send_planes)
 
@@ -284,8 +302,8 @@
         outs, halos = [], []
         rows = pl.ds(row, STEP)
         low, high = (
-            [embed(t) * keep for t in unpack([ref[rows, cols(i)] for i in range(SENT)])]
-            for ref, keep in ((packed_lo, keep_lo), (packed_hi, keep_hi))
+            [embed(t) for t in unpack([ref[rows, cols(i)] for i in range(SENT)])]
+            for ref in (packed_lo, packed_hi)
         )
         for j in range(TILES):
             at = (rows, cols(j))
@@ -329,8 +347,8 @@
         outs, marks = [], []
         for j in range(TILES):
             at = (pl.ds(row, STEP), cols(j))
-            d_lo = recv_lo1[at].astype(jnp.float32) * keep_lo
-            d_hi = recv_hi1[at].astype(jnp.float32) * keep_hi
+            d_lo = recv_lo1[at].astype(jnp.float32)
+            d_hi = recv_hi1[at].astype(jnp.float32)
             mine = [l1_ref[(k,) + at] for k in range(DEPTH)]
             outs.append(depth_max5([
                 jnp.where(d_lo == 2.0, ROOT, f_ref[(0,) + at]),
@@ -378,8 +396,8 @@
         outs = []
         for j in range(TILES):
             at = (pl.ds(row, STEP), cols(j))
-            d_lo = recv_lo2[at].astype(jnp.float32) * keep_lo
-            d_hi = recv_hi2[at].astype(jnp.float32) * keep_hi
+            d_lo = recv_lo2[at].astype(jnp.float32)
+            d_hi = recv_hi2[at].astype(jnp.float32)
             gone = gone_ref[at]
 
             def halo(k, bit, is_root):
@@ -395,7 +413,7 @@
         return lambda: put(row, outs, sides)
 
     def second3(row):
-        flags, words = [], []
+        flags = []
         for j in range(TILES):
             at = (pl.ds(row, STEP), cols(j))
             word = None
@@ -405,9 +423,7 @@
                 state = jnp.where(root, 1 << 2 * k, jnp.where(near, 2 << 2 * k, 0))
                 word = state if word is None else word | state
                 flags.append(jnp.where(root | near, 0, 1))
-            words.append(word)
-        for j, t in enumerate(natural(words)):
-            st_ref[pl.ds(row, STEP), cols(j)] = t
+            st_ref[at] = word
         add_count(2, flags)
 
     rounds(first3, second3, lambda c: wait_recv(roots2(c)), lambda c: store(c).start())
@@ -425,13 +441,15 @@
             )
             for o, other in enumerate(group)
         ]
-        start(copies)
+        for copy in copies:
+            copy.start()
         total = part[stage]
         for o, copy in enumerate(copies):
             copy.wait_recv()
             total = total + parts[slot + o]
         part[stage + 1] = total
-        wait_send(copies)
+        for copy in copies:
+            copy.wait_send()
         slot += len(group)
     for k in range(3):
         count_ref[k] = jnp.sum(part[len(GROUPS), k:k + 1, :])
@@ -446,9 +464,9 @@
 
 
 def expand(word_ref, count_ref, out_ref, count_out_ref):
-    words = word_ref[...]
-    for k in range(DEPTH):
-        out_ref[k] = jnp.right_shift(words, 2 * k) & 3
+    for j, words in enumerate(natural([word_ref[:, cols(j)] for j in range(TILES)])):
+        for k in range(DEPTH):
+            out_ref[k, :, cols(j)] = jnp.right_shift(words, 2 * k) & 3
     for k in range(3):
         count_out_ref[k] = count_ref[k]
 

time: 62.3 us -> 59.6 us (0.957)
  Pallas kernels: 61.5 us -> 58.8 us
    pallas_call x1, Pallas kernels: 58.3 us -> 55.3 us  [shards(): pl.pallas_call(functools.partial(kernel, n), out_shape=(jax.ShapeDtypeStr...]
where the time goes in v3:
time: 59.6 us; the launch traced here: 59.5 us
  Pallas kernels  58.8 us (99%)
  between operations  0.64 us (1%)
    pallas_call x1, Pallas kernels, shards(): pl.pallas_call(functools.partial(kernel, n), out_shape=(jax.ShapeDtypeStr...  55.3 us
    pallas_call x1, Pallas kernels, shards(): pl.pallas_call(expand, out_shape=(jax.ShapeDtypeStruct(slab, jnp.int32),...  3.56 us

profile of v3, /device:TPU:1, one launch (start us, length us, event | category | flops | bytes accessed | tf_op | source)
XLA Modules:
  0.0 59.5 jit_solution(3332603742098613953)
XLA Ops:
  0.6 55.3 %shard_map.30 = (s32[512,512]{1,0:T(8,128)}, s32[3]{0:T(128)}) custom-call(s32[4,512,512]{2,1,0:T(8,128)} %x_ref.1), custom_call_target="tpu_custom_call" | custom-call | tf_op jit(solution)/shard_map/pallas_call | solution.py:478
  55.9 3.6 %shard_map.31 = (s32[4,512,512]{2,1,0:T(8,128)}, s32[3]{0:T(128)}) custom-call(s32[512,512]{1,0:T(8,128)} %get-tuple-element.4.word_ref, s32[3]{0:T(128)} %get-tuple-element.5.count_ref), custom_call_target="tpu_custom_call" | custom-call | tf_op jit(solution)/shard_map/pallas_call | solution.py:514

commit v4 on v3

--- a/solution.py
+++ b/solution.py
@@ -275,9 +275,8 @@
             arrive(c)
 
             def body(row):
-                finish = first(row)
+                first(row)()
                 second(pl.multiple_of(row - CHUNK, STEP))
-                finish()
             over_rows(c, body)
             leave(c - 1)
         loop(1, CHUNKS, step)

time: 59.6 us -> 59.3 us (level)
  no operation moved by 1% of the time
where the time goes in v4:
time: 59.3 us; the launch traced here: 59.1 us
  Pallas kernels  58.5 us (99%)
  between operations  0.64 us (1%)
    pallas_call x1, Pallas kernels, shards(): pl.pallas_call(functools.partial(kernel, n), out_shape=(jax.ShapeDtypeStr...  54.9 us
    pallas_call x1, Pallas kernels, shards(): pl.pallas_call(expand, out_shape=(jax.ShapeDtypeStruct(slab, jnp.int32),...  3.56 us

profile of v4, /device:TPU:1, one launch (start us, length us, event | category | flops | bytes accessed | tf_op | source)
XLA Modules:
  0.0 59.1 jit_solution(9122289149596723864)
XLA Ops:
  0.6 54.9 %shard_map.30 = (s32[512,512]{1,0:T(8,128)}, s32[3]{0:T(128)}) custom-call(s32[4,512,512]{2,1,0:T(8,128)} %x_ref.1), custom_call_target="tpu_custom_call" | custom-call | tf_op jit(solution)/shard_map/pallas_call | solution.py:477
  55.6 3.6 %shard_map.31 = (s32[4,512,512]{2,1,0:T(8,128)}, s32[3]{0:T(128)}) custom-call(s32[512,512]{1,0:T(8,128)} %get-tuple-element.4.word_ref, s32[3]{0:T(128)} %get-tuple-element.5.count_ref), custom_call_target="tpu_custom_call" | custom-call | tf_op jit(solution)/shard_map/pallas_call | solution.py:513

commit v5 on v4

--- a/solution.py
+++ b/solution.py
@@ -212,7 +212,6 @@
     def over_rows(c, body):
         loop(0, CHUNK // STEP, lambda i: body(pl.multiple_of(c * CHUNK + i * STEP, STEP)))
 
-    loop(0, CHUNKS, lambda c: load(c).start())
     barrier = pltpu.get_barrier_semaphore()
 
     def greet(other):
@@ -222,6 +221,7 @@
     greeted = [p for group in partners for p in group]
     for other in greeted:
         greet(other)
+    loop(0, CHUNKS, lambda c: load(c).start())
 
     def outside(*refs):
         def fill():

time: 59.3 us -> 59.1 us (level)
  no operation moved by 1% of the time
where the time goes in v5:
time: 59.1 us; the launch traced here: 59 us
  Pallas kernels  58.4 us (99%)
  between operations  0.64 us (1%)
    pallas_call x1, Pallas kernels, shards(): pl.pallas_call(functools.partial(kernel, n), out_shape=(jax.ShapeDtypeStr...  54.8 us
    pallas_call x1, Pallas kernels, shards(): pl.pallas_call(expand, out_shape=(jax.ShapeDtypeStruct(slab, jnp.int32),...  3.56 us

profile of v5, /device:TPU:1, one launch (start us, length us, event | category | flops | bytes accessed | tf_op | source)
XLA Modules:
  0.0 59.0 jit_solution(12870925590195869631)
XLA Ops:
  0.6 54.8 %shard_map.30 = (s32[512,512]{1,0:T(8,128)}, s32[3]{0:T(128)}) custom-call(s32[4,512,512]{2,1,0:T(8,128)} %x_ref.1), custom_call_target="tpu_custom_call" | custom-call | tf_op jit(solution)/shard_map/pallas_call | solution.py:477
  55.4 3.6 %shard_map.31 = (s32[4,512,512]{2,1,0:T(8,128)}, s32[3]{0:T(128)}) custom-call(s32[512,512]{1,0:T(8,128)} %get-tuple-element.4.word_ref, s32[3]{0:T(128)} %get-tuple-element.5.count_ref), custom_call_target="tpu_custom_call" | custom-call | tf_op jit(solution)/shard_map/pallas_call | solution.py:513
